TPU v7x, 32 devices: a whole 2x2x4 slice. The times are simulated.
32 devices in a mesh: row: 8 (over y, x, core), col: 4 (over z).
Axes of the slice: x: 2, y: 2, z: 4, core: 2. Of those that a mesh axis runs over, the one named last changes fastest.
Arguments:
- window_rows: bfloat16 [1024, 65536], P('row', 'col'), may hold values from -6 to 6
- omega_cols: bfloat16 [512, 1024], P(None, 'row'), may hold values from -0.1875 to 0.1875
- psi_rows: bfloat16 [65536, 1024], P(('col', 'row')), may hold values from -0.046875 to 0.046875
- upsilon_rows: bfloat16 [65536, 2048], P(('col', 'row')), may hold values from -0.046875 to 0.046875
- phi_cols: bfloat16 [2048, 1024], P(None, 'row'), may hold values from -0.1875 to 0.1875
- range_old: float32 [512, 65536], P(None, ('col', 'row')), may hold values from -6 to 6
- core_old: float32 [2048, 2048], P('row', 'col'), may hold values from -6 to 6
Outputs:
- range_sketch: float32 [512, 65536], P(None, ('col', 'row'))
- corange_sketch: float32 [1024, 1024], P('row', 'col')
- core_sketch: float32 [2048, 2048], P('row', 'col')
All inputs are finite; a program needn't handle non-finite values.
Results may differ from a plain program's by a relative error of at most 0.0022.
Values may be sent and summed in bfloat16 or wider, within the bound.
A program may use at most 128 MiB of HBM per device.

v0:
```python
import jax
import jax.numpy as jnp
from jax import lax
from jax.sharding import PartitionSpec as P


def shards(window_rows, omega_cols, psi_rows, upsilon_rows, phi_cols, range_old, core_old):
    relaid = lax.all_to_all(window_rows, "row", split_axis=1, concat_axis=0, tiled=True)
    range_sketch = range_old + jnp.dot(
        lax.all_gather(omega_cols, "row", axis=1, tiled=True),
        relaid,
        preferred_element_type=jnp.float32,
    )
    co_part = jnp.dot(relaid, psi_rows, preferred_element_type=jnp.float32)
    core_part = jnp.dot(relaid, upsilon_rows, preferred_element_type=jnp.float32)
    rows_sum = (
        lax.psum_scatter(co_part, "row", scatter_dimension=0, tiled=True),
        lax.psum_scatter(core_part, "row", scatter_dimension=0, tiled=True),
    )
    corange_sketch, sketched = (
        lax.psum_scatter(rows_sum[0], "col", scatter_dimension=1, tiled=True),
        lax.psum_scatter(rows_sum[1], "col", scatter_dimension=1, tiled=True),
    )
    sketched = sketched.astype(jnp.bfloat16)
    core_term = jnp.dot(phi_cols, sketched, preferred_element_type=jnp.float32)
    core_sketch = core_old + lax.psum_scatter(core_term, "row", scatter_dimension=0, tiled=True)
    return (range_sketch, corange_sketch, core_sketch)


def solution(mesh):
    placed = (
        P("row", "col"),
        P(None, "row"),
        P(("col", "row"), None),
        P(("col", "row"), None),
        P(None, "row"),
        P(None, ("col", "row")),
        P("row", "col"),
    )
    return jax.shard_map(
        shards,
        mesh=mesh,
        in_specs=placed,
        out_specs=(P(None, ("col", "row")), P("row", "col"), P("row", "col")),
        check_vma=False,
    )
```

profile of v0, /device:TPU:11, one launch (start us, length us, event | category | flops | bytes accessed | tf_op | source)
XLA Modules:
  0.0 349.0 jit_solution(8678453194813222285)
XLA Ops:
  7.2 0.0 copy-start
  7.2 0.0 reduce-scatter.10.cloned.1.call-start
  7.2 6.4 %copy.14 = bf16[128,16384]{0,1:T(8,128)(2,1)} copy(bf16[128,16384]{1,0:T(8,128)(2,1)} %param.7) | data formatting | bytes 8388608 | tf_op args[0]
  13.6 52.6 %all_to_all.19 = bf16[128,8,2048]{0,2,1:T(8,128)(2,1)} all-to-all(bf16[128,8,2048]{0,2,1:T(8,128)(2,1)} %bitcast.13), channel_id=1, replica_groups=mesh['row'=8,'col'=4] {'row'}, dimensions={1} | all-to-all | bytes 8388608 | tf_op jit(solution)/shard_map/all_to_all | solution.py:8
  66.3 6.5 %copy.15 = bf16[8,128,2048]{2,1,0:T(8,128)(2,1)} copy(bf16[8,128,2048]{1,2,0:T(8,128)(2,1)} %bitcast.12) | data formatting | bytes 8388608 | tf_op jit(solution)/shard_map/all_to_all | solution.py:8
  72.7 14.4 %fusion.2 = f32[1024,2048]{1,0:T(8,128)} fusion(bf16[1024,2048]{1,0:T(8,128)(2,1)} %bitcast.14, bf16[2048,2048]{1,0:T(8,128)(2,1)} %param.10), kind=kOutput, calls=%fused_computation.4 | convolution fusion | flops 8589934592 | bytes 20971520 | tf_op jit(solution)/shard_map/dot_general | solution.py:15
  87.2 0.0 reduce-scatter.10.cloned.1.call-update
  87.2 0.0 reduce-scatter.12.cloned.1.call-start
  87.2 71.6 %reduce-scatter.10.cloned.1.call-done = f32[128,2048]{1,0:T(8,128)} async-done(((f32[1024,2048]{1,0:T(8,128)}), f32[128,2048]{1,0:T(8,128)}) %reduce-scatter.10.cloned.1.call-update) | async-done | bytes 1048592 | tf_op jit(solution)/shard_map/reduce_scatter | solution.py:18
  158.8 0.0 reduce-scatter.12.cloned.1.call-update
  158.8 0.0 reduce-scatter.6.cloned.1.call-start
  158.9 10.0 %fusion.1 = f32[1024,1024]{1,0:T(8,128)} fusion(bf16[1024,2048]{1,0:T(8,128)(2,1)} %bitcast.15, bf16[2048,1024]{1,0:T(8,128)(2,1)} %param.9), kind=kOutput, calls=%fused_computation.3 | convolution fusion | flops 4294967296 | bytes 12582912 | tf_op jit(solution)/shard_map/dot_general | solution.py:14
  168.8 0.0 reduce-scatter.6.cloned.1.call-update
  168.9 0.0 all-gather.2.cloned.1.call-start
  168.9 0.5 all-gather.2.cloned.1.call-update
  169.4 0.0 copy-start.1
  169.5 0.0 reduce-scatter.14.cloned.1.call-start
  169.5 16.6 %reduce-scatter.12.cloned.1.call-done = f32[128,512]{1,0:T(8,128)} async-done(((f32[128,2048]{1,0:T(8,128)}), f32[128,512]{1,0:T(8,128)}) %reduce-scatter.12.cloned.1.call-update) | async-done | bytes 262160 | tf_op jit(solution)/shard_map/reduce_scatter | solution.py:22
  186.1 0.0 copy-done
  186.1 3.6 %convolution_bitcast_fusion = f32[2048,512]{0,1:T(8,128)} fusion(bf16[2048,128]{1,0:T(8,128)(2,1)S(1)} %copy-done, f32[128,512]{1,0:T(8,128)} %reduce-scatter.12.cloned.1.call-done), kind=kOutput, calls=%fused_computation | convolution fusion | flops 268500992 | bytes 4980736 | tf_op jit(solution)/shard_map/dot_general | solution.py:25
  189.7 0.0 reduce-scatter.14.cloned.1.call-update
  189.8 0.0 reduce-scatter.8.cloned.1.call-start
  189.8 52.2 %reduce-scatter.6.cloned.1.call-done = f32[128,1024]{1,0:T(8,128)} async-done(((f32[1024,1024]{1,0:T(8,128)}), f32[128,1024]{1,0:T(8,128)}) %reduce-scatter.6.cloned.1.call-update) | async-done | bytes 524304 | tf_op jit(solution)/shard_map/reduce_scatter | solution.py:17
  242.0 0.0 reduce-scatter.8.cloned.1.call-update
  242.1 0.0 copy-done.1
  242.1 0.2 copy.16
  242.3 25.6 %all-gather.2.cloned.1.call-done = bf16[512,1024]{1,0:T(8,128)(2,1)} async-done(((bf16[512,128]{1,0:T(8,128)(2,1)}), bf16[512,1024]{1,0:T(8,128)(2,1)}) %all-gather.2.cloned.1.call-update) | async-done | bytes 1048592 | tf_op jit(solution)/shard_map/all_gather | solution.py:10
  267.9 8.1 %convolution_add_fusion = f32[512,2048]{1,0:T(8,128)} fusion(f32[512,2048]{1,0:T(8,128)} %param.12, bf16[512,1024]{1,0:T(8,128)(2,1)} %all-gather.2.cloned.1.call-done, bf16[1024,2048]{1,0:T(8,128)(2,1)} %bitcast.16), kind=kOutput, calls=%fused_computation.1 | convolution fusion | flops 2148532224 | bytes 13631488 | tf_op jit(solution)/shard_map/dot_general | solution.py:9
  276.0 45.6 %reduce-scatter.14.cloned.1.call-done = f32[256,512]{0,1:T(8,128)} async-done(((f32[2048,512]{0,1:T(8,128)}), f32[256,512]{0,1:T(8,128)}) %reduce-scatter.14.cloned.1.call-update) | async-done | bytes 524304 | tf_op jit(solution)/shard_map/reduce_scatter | solution.py:26
  321.6 1.1 add.17
  322.7 1.0 copy.17
  323.7 18.4 %reduce-scatter.8.cloned.1.call-done = f32[128,256]{1,0:T(8,128)} async-done(((f32[128,1024]{1,0:T(8,128)}), f32[128,256]{1,0:T(8,128)}) %reduce-scatter.8.cloned.1.call-update) | async-done | bytes 131088 | tf_op jit(solution)/shard_map/reduce_scatter | solution.py:21
Async XLA Ops:
  7.2 179.0 %copy-start = (bf16[2048,128]{1,0:T(8,128)(2,1)S(1)}, bf16[2048,128]{1,0:T(8,128)(2,1)}, u32[]{:S(2)}) copy-start(bf16[2048,128]{1,0:T(8,128)(2,1)} %param.11) | copy-start | bytes 1572868
  7.2 151.6 %reduce-scatter.10.cloned.1.call-start = ((), (), s32[]{:S(2)}) async-start(), calls=%async_computation.9 | async-start | bytes 9437184 | tf_op jit(solution)/shard_map/reduce_scatter | solution.py:18
  87.2 98.9 %reduce-scatter.12.cloned.1.call-start = ((), (), s32[]{:S(2)}) async-start(), calls=%async_computation.10 | async-start | bytes 1310720 | tf_op jit(solution)/shard_map/reduce_scatter | solution.py:22
  158.8 83.2 %reduce-scatter.6.cloned.1.call-start = ((), (), s32[]{:S(2)}) async-start(), calls=%async_computation.7 | async-start | bytes 4718592 | tf_op jit(solution)/shard_map/reduce_scatter | solution.py:17
  168.9 99.0 %all-gather.2.cloned.1.call-start = ((), (), s32[]{:S(2)}) async-start(), calls=%async_computation.6 | async-start | bytes 1179648 | tf_op jit(solution)/shard_map/all_gather | solution.py:10
  169.4 72.6 %copy-start.1 = (f32[256,512]{1,0:T(8,128)S(1)}, f32[256,512]{1,0:T(8,128)}, u32[]{:S(2)}) copy-start(f32[256,512]{1,0:T(8,128)} %param.13) | copy-start | bytes 1572868
  169.5 152.1 %reduce-scatter.14.cloned.1.call-start = ((), (), s32[]{:S(2)}) async-start(), calls=%async_computation.11 | async-start | bytes 4718592 | tf_op jit(solution)/shard_map/reduce_scatter | solution.py:26
  189.8 152.4 %reduce-scatter.8.cloned.1.call-start = ((), (), s32[]{:S(2)}) async-start(), calls=%async_computation.8 | async-start | bytes 655360 | tf_op jit(solution)/shard_map/reduce_scatter | solution.py:21
Sparse Core Ops, SparseCore 0:
  87.3 71.4 reduce-scatter.9
  161.1 24.9 reduce-scatter.11
  190.1 51.9 reduce-scatter.5
  243.8 24.0 all-gather.1
  271.1 50.4 reduce-scatter.13
  324.3 17.8 reduce-scatter.7
where the time goes:
time: 355 us; the launch traced here: 349 us
  waiting for transfers between devices  231 us (65%)
  blocking collectives  52.6 us (15%)
  matrix products  36.2 us (10%)
  local copies, waits for them, and re-layouts  14.1 us (4%)
  between operations  14.1 us (4%)
    reduce_scatter x1, waiting for transfers between devices, shards(): lax.psum_scatter(core_part, 'row', scatter_dimension=0, tiled=True)  71.6 us
    all_to_all x1, blocking collectives, shards(): lax.all_to_all(window_rows, 'row', split_axis=1, concat_axis=0, tiled=True)  52.6 us
    reduce_scatter x1, waiting for transfers between devices, shards(): lax.psum_scatter(co_part, 'row', scatter_dimension=0, tiled=True)  52.2 us
    reduce_scatter x1, waiting for transfers between devices, shards(): lax.psum_scatter(core_term, 'row', scatter_dimension=0, tiled=True)  45.6 us
    all_gather x1, waiting for transfers between devices, shards(): lax.all_gather(omega_cols, 'row', axis=1, tiled=True)  25.6 us
    reduce_scatter x1, waiting for transfers between devices, shards(): lax.psum_scatter(rows_sum[0], 'col', scatter_dimension=1, tiled=True)  18.4 us
    reduce_scatter x1, waiting for transfers between devices, shards(): lax.psum_scatter(rows_sum[1], 'col', scatter_dimension=1, tiled=True)  16.6 us
    dot_general x1, matrix products, shards(): jnp.dot(relaid, upsilon_rows, preferred_element_type=jnp.float32)  14.4 us
  transfers between devices with their start and end apart: 6, of which 6 were waited for; matrix products, arithmetic and copies ran while one was open for 7% of the time, Pallas kernels for 0%

commit v1 on v0

v1 whole, which is shorter than its diff:
```python
import functools

import jax
import jax.numpy as jnp
from jax import lax
from jax.experimental import pallas as pl
from jax.experimental.pallas import tpu as pltpu
from jax.sharding import PartitionSpec as P

MESH = pl.DeviceIdType.MESH
LIMIT = 60 * 1024 * 1024


def greet(peers):
    barrier = pltpu.get_barrier_semaphore()
    for peer in peers:
        pl.semaphore_signal(barrier, inc=1, device_id=peer, device_id_type=MESH)
    pl.semaphore_wait(barrier, len(peers))


def send(src, dst, send_sem, recv_sem, peer):
    copy = pltpu.make_async_remote_copy(
        src_ref=src, dst_ref=dst, send_sem=send_sem, recv_sem=recv_sem, device_id=peer, device_id_type=MESH
    )
    copy.start()
    return copy


def exchange(n, window, phi, relaid, phi_all, keep_w, keep_p, send_sem, recv_sem, local_sem):
    me = lax.axis_index("row")
    rows, width = window.shape[0], relaid.shape[1]
    core_rows, depth = phi_all.shape[0], phi.shape[1]
    peers = [lax.rem(me + d, n) for d in range(1, n)]
    greet([{"row": p} for p in peers])
    copies = []
    for d, p in enumerate(peers):
        copies.append(send(
            window.at[:, pl.ds(pl.multiple_of(p * width, width), width)],
            relaid.at[pl.ds(pl.multiple_of(me * rows, rows), rows), :],
            send_sem.at[0, d], recv_sem.at[0, d], {"row": p}))
    for d, p in enumerate(peers):
        copies.append(send(
            phi.at[pl.ds(pl.multiple_of(p * core_rows, core_rows), core_rows), :],
            phi_all.at[:, pl.ds(pl.multiple_of(me * depth, depth), depth)],
            send_sem.at[1, d], recv_sem.at[1, d], {"row": p}))
    ins = (
        pltpu.make_async_copy(window.at[:, pl.ds(pl.multiple_of(me * width, width), width)], keep_w, local_sem.at[0]),
        pltpu.make_async_copy(phi.at[pl.ds(pl.multiple_of(me * core_rows, core_rows), core_rows), :], keep_p, local_sem.at[1]),
    )
    for c in ins:
        c.start()
    for c in ins:
        c.wait()
    outs = (
        pltpu.make_async_copy(keep_w, relaid.at[pl.ds(pl.multiple_of(me * rows, rows), rows), :], local_sem.at[2]),
        pltpu.make_async_copy(keep_p, phi_all.at[:, pl.ds(pl.multiple_of(me * depth, depth), depth)], local_sem.at[3]),
    )
    for c in outs:
        c.start()
    for c in outs:
        c.wait()
    for c in copies:
        c.wait()


def reduce_kernel(n, m, sk, co, gathered, co_out, *scratch):
    (acc_sk, acc_co, *recv), rest = scratch[:2 + 2 * (n.bit_length() - 1)], scratch[2 + 2 * (n.bit_length() - 1):]
    fin_sk, fin_co, z_sk, z_co, mine, load_sem, ss, rs, zs, zr, gs, gr, ls = rest
    levels = n.bit_length() - 1
    me, c = lax.axis_index("row"), lax.axis_index("col")
    bits = [(me // (1 << b)) % 2 for b in range(levels)]
    partner = [{"row": me + (1 - 2 * bits[b]) * (1 << b)} for b in range(levels)]
    row_peers = [lax.rem(me + d, n) for d in range(1, n)]
    col_peers = [lax.rem(c + d, m) for d in range(1, m)]
    greet([{"row": p} for p in row_peers] + [{"col": p} for p in col_peers])

    pieces = []
    low, high = list(range(1, levels)), list(range(levels - 1, 0, -1))
    for k, (src, acc, fin) in enumerate(((sk, acc_sk, fin_sk), (co, acc_co, fin_co))):
        half = src.shape[-1] // 2
        for h, order in enumerate((low, high)):
            pieces.append((src, acc, recv[k::2], fin, pl.ds(h * half, half), order))

    copies = []
    first = []
    for q, (src, acc, got, fin, cols, order) in enumerate(pieces):
        mine_first = []
        for i in range(n // 2):
            mine_first.append(send(
                src.at[i, 1 - bits[0], :, cols], got[0].at[i, :, cols], ss.at[q, 0, i], rs.at[q, 0, i], partner[0]))
        first.append(mine_first)
    loads = []
    for q, (src, acc, got, fin, cols, order) in enumerate(pieces):
        load = pltpu.make_async_copy(src.at[:, bits[0], :, cols], acc.at[:, :, cols], load_sem.at[q])
        load.start()
        loads.append(load)

    live = []
    for q, (src, acc, got, fin, cols, order) in enumerate(pieces):
        loads[q].wait()
        live.append((0, n // 2, 1))
        for i in range(n // 2):
            first[q][i].wait_recv()
            acc[i, :, cols] += got[0][i, :, cols]
        copies += first[q]
        if levels > 1:
            pass

    def at(base, stride, i):
        return base + stride * i

    for step in range(levels - 1):
        started = []
        for q, (src, acc, got, fin, cols, order) in enumerate(pieces):
            base, count, stride = live[q]
            bit = bits[order[step]]
            if order is not high and order == low:
                keep = (base + stride * bit, count // 2, stride * 2)
                give = (base + stride * (1 - bit), count // 2, stride * 2)
            else:
                keep = (base + stride * (count // 2) * bit, count // 2, stride)
                give = (base + stride * (count // 2) * (1 - bit), count // 2, stride)
            sent = []
            for i in range(count // 2):
                sent.append(send(
                    acc.at[at(give[0], give[2], i), :, cols], got[step + 1].at[i, :, cols],
                    ss.at[q, step + 1, i], rs.at[q, step + 1, i], partner[order[step]]))
            started.append(sent)
            live[q] = keep
        for q, (src, acc, got, fin, cols, order) in enumerate(pieces):
            base, count, stride = live[q]
            for i in range(count):
                started[q][i].wait_recv()
                j = at(base, stride, i)
                acc[j, :, cols] += got[step + 1][i, :, cols]
            copies += started[q]
    for q, (src, acc, got, fin, cols, order) in enumerate(pieces):
        fin[:, cols] = acc[live[q][0], :, cols]

    across = []
    for k, (fin, z) in enumerate(((fin_sk, z_sk), (fin_co, z_co))):
        width = z.shape[-1]
        across.append([
            send(fin.at[:, pl.ds(pl.multiple_of(p * width, width), width)], z.at[d], zs.at[k, d], zr.at[k, d], {"col": p})
            for d, p in enumerate(col_peers)])
    sums = []
    for k, (fin, z) in enumerate(((fin_sk, z_sk), (fin_co, z_co))):
        width = z.shape[-1]
        own = pl.ds(pl.multiple_of(c * width, width), width)
        for copy in across[k]:
            copy.wait_recv()
        total = fin[:, own]
        for d in range(m - 1):
            total = total + z[d]
        if k == 0:
            mine[...] = total.astype(mine.dtype)
            rows = mine.shape[0]
            place = gathered.at[pl.ds(pl.multiple_of(me * rows, rows), rows), :]
            spread = [
                send(mine, place, gs.at[d], gr.at[d], {"row": p}) for d, p in enumerate(row_peers)]
            put = pltpu.make_async_copy(mine, place, ls)
            put.start()
        else:
            co_out[...] = total
        copies += across[k]
    put.wait()
    for copy in spread:
        copy.wait()
    for copy in copies:
        copy.wait_send()


def shards(n, m, window_rows, omega_cols, psi_rows, upsilon_rows, phi_cols, range_old, core_old):
    any_space = pl.BlockSpec(memory_space=pl.ANY)
    vmem = pl.BlockSpec(memory_space=pltpu.VMEM)
    dma = pltpu.SemaphoreType.DMA
    rows, wide = window_rows.shape
    own = wide // n
    core_rows = phi_cols.shape[0] // n
    bf16, f32 = jnp.bfloat16, jnp.float32
    relaid, phi_all = pl.pallas_call(
        functools.partial(exchange, n),
        out_shape=(jax.ShapeDtypeStruct((rows * n, own), bf16), jax.ShapeDtypeStruct((core_rows, rows * n), bf16)),
        in_specs=[any_space] * 2,
        out_specs=(any_space, any_space),
        scratch_shapes=[
            pltpu.VMEM((rows, own), bf16), pltpu.VMEM((core_rows, rows), bf16),
            dma((2, n - 1)), dma((2, n - 1)), dma((4,)),
        ],
        compiler_params=pltpu.CompilerParams(collective_id=0, has_side_effects=True),
        name="exchange",
    )(window_rows, phi_cols)
    omega = lax.all_gather(omega_cols, "row", axis=1, tiled=True)
    core_part = jnp.dot(relaid, upsilon_rows, preferred_element_type=f32)
    co_part = jnp.dot(relaid, psi_rows, preferred_element_type=f32)
    s, l = core_part.shape[1], co_part.shape[1]
    levels = n.bit_length() - 1
    scratch = [pltpu.VMEM((n // 2, rows, s), f32), pltpu.VMEM((n // 2, rows, l), f32)]
    for b in range(levels):
        scratch += [pltpu.VMEM((n >> (b + 1), rows, s), f32), pltpu.VMEM((n >> (b + 1), rows, l), f32)]
    scratch += [
        pltpu.VMEM((rows, s), f32), pltpu.VMEM((rows, l), f32),
        pltpu.VMEM((m - 1, rows, s // m), f32), pltpu.VMEM((m - 1, rows, l // m), f32),
        pltpu.VMEM((rows, s // m), bf16), dma((4,)),
        dma((4, levels, n // 2)), dma((4, levels, n // 2)),
        dma((2, m - 1)), dma((2, m - 1)), dma((n - 1,)), dma((n - 1,)), dma,
    ]
    gathered, corange_sketch = pl.pallas_call(
        functools.partial(reduce_kernel, n, m),
        out_shape=(jax.ShapeDtypeStruct((rows * n, s // m), bf16), jax.ShapeDtypeStruct((rows, l // m), f32)),
        in_specs=[any_space] * 2,
        out_specs=(any_space, vmem),
        scratch_shapes=scratch,
        compiler_params=pltpu.CompilerParams(collective_id=1, has_side_effects=True, vmem_limit_bytes=LIMIT),
        name="reduce",
    )(core_part.reshape(n // 2, 2, rows, s), co_part.reshape(n // 2, 2, rows, l))
    range_sketch = range_old + jnp.dot(omega, relaid, preferred_element_type=f32)
    core_sketch = core_old + jnp.dot(phi_all, gathered, preferred_element_type=f32)
    return (range_sketch, corange_sketch, core_sketch)


def solution(mesh):
    placed = (
        P("row", "col"),
        P(None, "row"),
        P(("col", "row"), None),
        P(("col", "row"), None),
        P(None, "row"),
        P(None, ("col", "row")),
        P("row", "col"),
    )
    return jax.shard_map(
        functools.partial(shards, mesh.shape["row"], mesh.shape["col"]),
        mesh=mesh,
        in_specs=placed,
        out_specs=(P(None, ("col", "row")), P("row", "col"), P("row", "col")),
        check_vma=False,
    )
```

time: 355 us -> 227 us (0.64); the launches traced: 349 us -> 226 us
  waiting for transfers between devices: 231 us -> 0.68 us
  Pallas kernels: 0 us -> 170 us
  blocking collectives: 52.6 us -> 0 us
  matrix products: 36.2 us -> 30.5 us
    reduce_scatter x5 -> x0, waiting for transfers between devices: 204 us -> none  [the longest x1 71.6 us: shards(): lax.psum_scatter(core_part, 'row', scatter_dimension=0, tiled=True)]
    pallas_call x0 -> x2, Pallas kernels: none -> 170 us  [the longest x1 110 us: shards(): pl.pallas_call(functools.partial(reduce_kernel, n, m), out_shape=(jax.Sha...]
    all_to_all x1 -> x0, blocking collectives: 52.6 us -> none  [shards(): lax.all_to_all(window_rows, 'row', split_axis=1, concat_axis=0, tiled=True)]
    all_gather x1, waiting for transfers between devices: 25.6 us -> 0.01 us  [shards(): omega = lax.all_gather(omega_cols, 'row', axis=1, tiled=True)]
    all_to_all x1 -> x0, local copies, waits for them, and re-layouts: 6.47 us -> none  [shards(): lax.all_to_all(window_rows, 'row', split_axis=1, concat_axis=0, tiled=True)]
    dot_general x4, matrix products: 36.2 us -> 30.5 us  [the longest x1 11.1 us: shards(): core_part = jnp.dot(relaid, upsilon_rows, preferred_element_type=f32)]
    unnamed x7 -> x15, local copies, waits for them, and re-layouts: 7.62 us -> 11.5 us
  transfers between devices with their start and end apart: 6 -> 1, of which waited for: 6 -> 0; matrix products, arithmetic and copies ran while one was open for 7% -> 12% of each run, Pallas kernels for 0% -> 75%
where the time goes in v1:
time: 227 us; the launch traced here: 226 us
  Pallas kernels  170 us (75%)
  matrix products  30.5 us (13%)
  between operations  14.1 us (6%)
  local copies, waits for them, and re-layouts  11.5 us (5%)
    pallas_call x1, Pallas kernels, shards(): pl.pallas_call(functools.partial(reduce_kernel, n, m), out_shape=(jax.Sha...  110 us
    pallas_call x1, Pallas kernels, shards(): pl.pallas_call(functools.partial(exchange, n), out_shape=(jax.ShapeDtypeS...  59.4 us
    unnamed x15, local copies, waits for them, and re-layouts  11.5 us
    dot_general x1, matrix products, shards(): core_part = jnp.dot(relaid, upsilon_rows, preferred_element_type=f32)  11.1 us
    dot_general x1, matrix products, shards(): co_part = jnp.dot(relaid, psi_rows, preferred_element_type=f32)  10.1 us
    dot_general x1, matrix products, shards(): jnp.dot(omega, relaid, preferred_element_type=f32)  8.12 us
  transfers between devices with their start and end apart: 1, of which 0 were waited for; matrix products, arithmetic and copies ran while one was open for 12% of the time, Pallas kernels for 75%

profile of v1, /device:TPU:11, one launch (start us, length us, event | category | flops | bytes accessed | tf_op | source)
XLA Modules:
  0.0 226.4 jit_solution(8743352591108199385)
XLA Ops:
  7.2 0.0 all-gather.2.cloned.1.call-start
  7.2 0.7 all-gather.2.cloned.1.call-update
  7.9 59.4 %exchange.1 = (bf16[1024,2048]{1,0:T(8,128)(2,1)}, bf16[256,1024]{1,0:T(8,128)(2,1)}) custom-call(bf16[128,16384]{1,0:T(8,128)(2,1)} %window.1, bf16[2048,128]{1,0:T(8,128)(2,1)} %phi.1), custom_call_target="tpu_custom_call" | custom-call | tf_op jit(solution)/shard_map/exchange/pallas_call | solution.py:181
  67.4 0.0 copy-start.4
  67.4 0.0 copy-start.5
  67.4 10.1 %fusion.1 = f32[1024,1024]{1,0:T(8,128)} fusion(bf16[1024,2048]{1,0:T(8,128)(2,1)} %get-tuple-element.7, bf16[2048,1024]{1,0:T(8,128)(2,1)} %param.9), kind=kOutput, calls=%fused_computation.3 | convolution fusion | flops 4294967296 | bytes 12582912 | tf_op jit(solution)/shard_map/dot_general | solution.py:195
  77.5 0.0 copy-done.4
  77.5 0.0 copy-done.5
  77.5 11.1 %fusion = f32[1024,2048]{1,0:T(8,128)} fusion(bf16[1024,2048]{1,0:T(8,128)(2,1)S(1)} %copy-done.5, bf16[2048,2048]{1,0:T(8,128)(2,1)S(1)} %copy-done.4), kind=kOutput, calls=%fused_computation.2 | convolution fusion | flops 8589934592 | bytes 20971520 | tf_op jit(solution)/shard_map/dot_general | solution.py:194
  88.6 110.1 %reduce.1 = (bf16[1024,512]{1,0:T(8,128)(2,1)}, f32[128,256]{1,0:T(8,128)}) custom-call(f32[4,2,128,2048]{3,2,1,0:T(8,128)} %bitcast.12, f32[4,2,128,1024]{3,2,1,0:T(8,128)} %bitcast.13), custom_call_target="tpu_custom_call" | custom-call | tf_op jit(solution)/shard_map/reduce/pallas_call | solution.py:208
  198.6 0.0 copy-start
  198.6 0.0 copy-start.1
  198.7 0.0 copy-start.2
  198.7 5.5 %copy.10 = f32[512,2048]{0,1:T(8,128)} copy(f32[512,2048]{1,0:T(8,128)} %param.12) | data formatting | bytes 8388608 | tf_op args[5]
  204.2 0.0 copy-done
  204.2 0.0 copy-done.1
  204.2 0.0 copy-done.2
  204.2 1.2 convolution_add_fusion
  205.4 0.0 all-gather.2.cloned.1.call-done
  205.4 8.1 %bitcast_add_fusion = f32[512,2048]{0,1:T(8,128)} fusion(f32[512,2048]{0,1:T(8,128)} %copy.10, bf16[1024,2048]{1,0:T(8,128)(2,1)} %get-tuple-element.7, bf16[512,1024]{1,0:T(8,128)(2,1)} %all-gather.2.cloned.1.call-done), kind=kOutput, calls=%fused_computation | convolution fusion | flops 2148532224 | bytes 13631488 | tf_op jit(solution)/shard_map/dot_general | solution.py:217
  213.5 0.0 copy-start.3
  213.5 5.4 %copy.11 = f32[512,2048]{1,0:T(8,128)} copy(f32[512,2048]{0,1:T(8,128)} %bitcast_add_fusion) | data formatting | bytes 8388608
  218.9 0.0 copy-done.3
  218.9 0.7 copy.13
Async XLA Ops:
  7.2 198.2 %all-gather.2.cloned.1.call-start = ((), (), s32[]{:S(2)}) async-start(), calls=%async_computation | async-start | bytes 1179648 | tf_op jit(solution)/shard_map/all_gather | solution.py:193
  67.4 10.1 %copy-start.4 = (bf16[2048,2048]{1,0:T(8,128)(2,1)S(1)}, bf16[2048,2048]{1,0:T(8,128)(2,1)}, u32[]{:S(2)}) copy-start(bf16[2048,2048]{1,0:T(8,128)(2,1)} %param.10) | copy-start | bytes 25165828
  67.4 10.1 %copy-start.5 = (bf16[1024,2048]{1,0:T(8,128)(2,1)S(1)}, bf16[1024,2048]{1,0:T(8,128)(2,1)}, u32[]{:S(2)}) copy-start(bf16[1024,2048]{1,0:T(8,128)(2,1)} %get-tuple-element.7) | copy-start | bytes 12582916
  198.6 5.5 %copy-start = (bf16[1024,512]{1,0:T(8,128)(2,1)S(1)}, bf16[1024,512]{1,0:T(8,128)(2,1)}, u32[]{:S(2)}) copy-start(bf16[1024,512]{1,0:T(8,128)(2,1)} %get-tuple-element.10) | copy-start | bytes 3145732
  198.6 5.5 %copy-start.1 = (f32[256,512]{1,0:T(8,128)S(1)}, f32[256,512]{1,0:T(8,128)}, u32[]{:S(2)}) copy-start(f32[256,512]{1,0:T(8,128)} %param.13) | copy-start | bytes 1572868
  198.7 5.5 %copy-start.2 = (bf16[256,1024]{1,0:T(8,128)(2,1)S(1)}, bf16[256,1024]{1,0:T(8,128)(2,1)}, u32[]{:S(2)}) copy-start(bf16[256,1024]{1,0:T(8,128)(2,1)} %get-tuple-element.9) | copy-start | bytes 1572868
  213.5 5.4 %copy-start.3 = (f32[128,256]{1,0:T(8,128)S(1)}, f32[128,256]{1,0:T(8,128)}, u32[]{:S(2)}) copy-start(f32[128,256]{1,0:T(8,128)} %get-tuple-element.18) | copy-start | bytes 393220
Sparse Core Ops, SparseCore 0:
  9.8 55.3 all-gather.1

commit v2 on v1

--- a/solution.py
+++ b/solution.py
@@ -84,66 +84,79 @@
     copies = []
     first = []
     for q, (src, acc, got, fin, cols, order) in enumerate(pieces):
-        mine_first = []
-        for i in range(n // 2):
-            mine_first.append(send(
-                src.at[i, 1 - bits[0], :, cols], got[0].at[i, :, cols], ss.at[q, 0, i], rs.at[q, 0, i], partner[0]))
-        first.append(mine_first)
+        first.append([
+            send(src.at[i, 1 - bits[0], :, cols], got[0].at[i, :, cols], ss.at[q, 0, i], rs.at[q, 0, i], partner[0])
+            for i in range(n // 2)])
     loads = []
     for q, (src, acc, got, fin, cols, order) in enumerate(pieces):
         load = pltpu.make_async_copy(src.at[:, bits[0], :, cols], acc.at[:, :, cols], load_sem.at[q])
         load.start()
         loads.append(load)
 
-    live = []
-    for q, (src, acc, got, fin, cols, order) in enumerate(pieces):
+    live = [(0, n // 2, 1)] * 4
+    started = [None] * 4
+
+    def pair(q):
+        src, acc, got, fin, cols, order = pieces[q]
         loads[q].wait()
-        live.append((0, n // 2, 1))
         for i in range(n // 2):
             first[q][i].wait_recv()
             acc[i, :, cols] += got[0][i, :, cols]
-        copies += first[q]
-        if levels > 1:
-            pass
-
-    def at(base, stride, i):
-        return base + stride * i
-
+        copies.extend(first[q])
+
+    def give(q, step):
+        src, acc, got, fin, cols, order = pieces[q]
+        base, count, stride = live[q]
+        bit, half = bits[order[step]], count // 2
+        if order is low:
+            live[q] = (base + stride * bit, half, stride * 2)
+            start, jump = base + stride * (1 - bit), stride * 2
+        else:
+            live[q] = (base + stride * half * bit, half, stride)
+            start, jump = base + stride * half * (1 - bit), stride
+        started[q] = [
+            send(acc.at[start + jump * i, :, cols], got[step + 1].at[i, :, cols],
+                 ss.at[q, step + 1, i], rs.at[q, step + 1, i], partner[order[step]])
+            for i in range(half)]
+
+    def take(q, step):
+        src, acc, got, fin, cols, order = pieces[q]
+        base, count, stride = live[q]
+        for i in range(count):
+            started[q][i].wait_recv()
+            if step == levels - 2:
+                fin[:, cols] = acc[base + stride * i, :, cols] + got[step + 1][i, :, cols]
+            else:
+                acc[base + stride * i, :, cols] += got[step + 1][i, :, cols]
+        copies.extend(started[q])
+
+    def cross(k):
+        fin, z = ((fin_sk, z_sk), (fin_co, z_co))[k]
+        width = z.shape[-1]
+        return [
+            send(fin.at[:, pl.ds(pl.multiple_of(p * width, width), width)], z.at[d], zs.at[k, d], zr.at[k, d], {"col": p})
+            for d, p in enumerate(col_peers)]
+
+    for q in (0, 1):
+        pair(q)
+        give(q, 0)
+    for q in (2, 3):
+        pair(q)
     for step in range(levels - 1):
-        started = []
-        for q, (src, acc, got, fin, cols, order) in enumerate(pieces):
-            base, count, stride = live[q]
-            bit = bits[order[step]]
-            if order is not high and order == low:
-                keep = (base + stride * bit, count // 2, stride * 2)
-                give = (base + stride * (1 - bit), count // 2, stride * 2)
-            else:
-                keep = (base + stride * (count // 2) * bit, count // 2, stride)
-                give = (base + stride * (count // 2) * (1 - bit), count // 2, stride)
-            sent = []
-            for i in range(count // 2):
-                sent.append(send(
-                    acc.at[at(give[0], give[2], i), :, cols], got[step + 1].at[i, :, cols],
-                    ss.at[q, step + 1, i], rs.at[q, step + 1, i], partner[order[step]]))
-            started.append(sent)
-            live[q] = keep
-        for q, (src, acc, got, fin, cols, order) in enumerate(pieces):
-            base, count, stride = live[q]
-            for i in range(count):
-                started[q][i].wait_recv()
-                j = at(base, stride, i)
-                acc[j, :, cols] += got[step + 1][i, :, cols]
-            copies += started[q]
-    for q, (src, acc, got, fin, cols, order) in enumerate(pieces):
-        fin[:, cols] = acc[live[q][0], :, cols]
-
-    across = []
-    for k, (fin, z) in enumerate(((fin_sk, z_sk), (fin_co, z_co))):
-        width = z.shape[-1]
-        across.append([
-            send(fin.at[:, pl.ds(pl.multiple_of(p * width, width), width)], z.at[d], zs.at[k, d], zr.at[k, d], {"col": p})
-            for d, p in enumerate(col_peers)])
-    sums = []
+        for q in (0, 1):
+            take(q, step)
+            if step < levels - 2:
+                give(q, step + 1)
+        if step == max(levels - 3, 0):
+            for q in (2, 3):
+                give(q, 0)
+    across = [cross(0)]
+    for step in range(levels - 1):
+        for q in (2, 3):
+            take(q, step)
+            if step < levels - 2:
+                give(q, step + 1)
+    across.append(cross(1))
     for k, (fin, z) in enumerate(((fin_sk, z_sk), (fin_co, z_co))):
         width = z.shape[-1]
         own = pl.ds(pl.multiple_of(c * width, width), width)
@@ -190,6 +203,7 @@
         compiler_params=pltpu.CompilerParams(collective_id=0, has_side_effects=True),
         name="exchange",
     )(window_rows, phi_cols)
+    relaid, omega_cols = lax.optimization_barrier((relaid, omega_cols))
     omega = lax.all_gather(omega_cols, "row", axis=1, tiled=True)
     core_part = jnp.dot(relaid, upsilon_rows, preferred_element_type=f32)
     co_part = jnp.dot(relaid, psi_rows, preferred_element_type=f32)

time: 227 us -> 192 us (0.85)
  Pallas kernels: 170 us -> 145 us
  local copies, waits for them, and re-layouts: 11.5 us -> 0.68 us
    pallas_call x1, Pallas kernels: 110 us -> 89.7 us  [shards(): pl.pallas_call(functools.partial(reduce_kernel, n, m), out_shape=(jax.Sha...]
    unnamed x15 -> x11, local copies, waits for them, and re-layouts: 11.5 us -> 0.68 us
    pallas_call x1, Pallas kernels: 59.4 us -> 55.2 us  [shards(): pl.pallas_call(functools.partial(exchange, n), out_shape=(jax.ShapeDtypeS...]
  transfers between devices with their start and end apart: 1 -> 1, of which waited for: 0 -> 0; matrix products, arithmetic and copies ran while one was open for 12% -> 12% of each run, Pallas kernels for 75% -> 47%
where the time goes in v2:
time: 192 us; the launch traced here: 191 us
  Pallas kernels  145 us (76%)
  matrix products  31.7 us (17%)
  between operations  14.1 us (7%)
    pallas_call x1, Pallas kernels, shards(): pl.pallas_call(functools.partial(reduce_kernel, n, m), out_shape=(jax.Sha...  89.7 us
    pallas_call x1, Pallas kernels, shards(): pl.pallas_call(functools.partial(exchange, n), out_shape=(jax.ShapeDtypeS...  55.2 us
    dot_general x1, matrix products, shards(): core_part = jnp.dot(relaid, upsilon_rows, preferred_element_type=f32)  11 us
    dot_general x1, matrix products, shards(): co_part = jnp.dot(relaid, psi_rows, preferred_element_type=f32)  10.1 us
    dot_general x1, matrix products, shards(): jnp.dot(omega, relaid, preferred_element_type=f32)  8.16 us
  transfers between devices with their start and end apart: 1, of which 0 were waited for; matrix products, arithmetic and copies ran while one was open for 12% of the time, Pallas kernels for 47%

profile of v2, /device:TPU:11, one launch (start us, length us, event | category | flops | bytes accessed | tf_op | source)
XLA Modules:
  0.0 191.5 jit_solution(16615213677621380337)
XLA Ops:
  7.2 0.0 all-gather.2.cloned.1.call-start
  7.2 55.2 %exchange.1 = (bf16[1024,2048]{1,0:T(8,128)(2,1)}, bf16[256,1024]{1,0:T(8,128)(2,1)}) custom-call(bf16[128,16384]{1,0:T(8,128)(2,1)} %window.1, bf16[2048,128]{1,0:T(8,128)(2,1)} %phi.1), custom_call_target="tpu_custom_call" | custom-call | tf_op jit(solution)/shard_map/exchange/pallas_call | solution.py:194
  62.4 0.0 all-gather.2.cloned.1.call-update
  62.5 0.0 copy-start.3
  62.5 0.0 copy-start.4
  62.5 10.1 %fusion.1 = f32[1024,1024]{1,0:T(8,128)} fusion(bf16[1024,2048]{1,0:T(8,128)(2,1)} %get-tuple-element.11, bf16[2048,1024]{1,0:T(8,128)(2,1)} %param.9), kind=kOutput, calls=%fused_computation.3 | convolution fusion | flops 4294967296 | bytes 12582912 | tf_op jit(solution)/shard_map/dot_general | solution.py:209
  72.6 0.0 copy-done.3
  72.6 0.0 copy-done.4
  72.6 11.0 %fusion = f32[1024,2048]{1,0:T(8,128)} fusion(bf16[1024,2048]{1,0:T(8,128)(2,1)S(1)} %copy-done.4, bf16[2048,2048]{1,0:T(8,128)(2,1)S(1)} %copy-done.3), kind=kOutput, calls=%fused_computation.2 | convolution fusion | flops 8589934592 | bytes 20971520 | tf_op jit(solution)/shard_map/dot_general | solution.py:208
  83.6 0.0 copy-start
  83.6 0.0 copy-start.1
  83.6 89.7 %reduce.1 = (bf16[1024,512]{1,0:T(8,128)(2,1)}, f32[128,256]{1,0:T(8,128)}) custom-call(f32[4,2,128,2048]{3,2,1,0:T(8,128)} %bitcast.10, f32[4,2,128,1024]{3,2,1,0:T(8,128)} %bitcast.11), custom_call_target="tpu_custom_call" | custom-call | tf_op jit(solution)/shard_map/reduce/pallas_call | solution.py:222
  173.3 0.0 copy-done
  173.3 0.0 copy-done.1
  173.3 2.5 %convolution_add_fusion.1 = f32[256,512]{1,0:T(8,128)} fusion(f32[256,512]{1,0:T(8,128)S(1)} %copy-done, bf16[256,1024]{1,0:T(8,128)(2,1)S(1)} %copy-done.1, bf16[1024,512]{1,0:T(8,128)(2,1)} %get-tuple-element.14), kind=kOutput, calls=%fused_computation.1 | convolution fusion | flops 268566528 | bytes 2621440 | tf_op jit(solution)/shard_map/dot_general | solution.py:232
  175.8 0.0 copy-start.2
  175.8 0.0 all-gather.2.cloned.1.call-done
  175.8 8.2 %convolution_add_fusion = f32[512,2048]{1,0:T(8,128)} fusion(f32[512,2048]{1,0:T(8,128)} %param.12, bf16[512,1024]{1,0:T(8,128)(2,1)} %all-gather.2.cloned.1.call-done, bf16[1024,2048]{1,0:T(8,128)(2,1)} %get-tuple-element.11), kind=kOutput, calls=%fused_computation | convolution fusion | flops 2148532224 | bytes 13631488 | tf_op jit(solution)/shard_map/dot_general | solution.py:231
  184.0 0.0 copy-done.2
  184.0 0.7 copy.11
Async XLA Ops:
  7.2 168.6 %all-gather.2.cloned.1.call-start = ((), (), s32[]{:S(2)}) async-start(), calls=%async_computation | async-start | bytes 1179648 | tf_op jit(solution)/shard_map/all_gather | solution.py:207
  62.5 10.1 %copy-start.3 = (bf16[2048,2048]{1,0:T(8,128)(2,1)S(1)}, bf16[2048,2048]{1,0:T(8,128)(2,1)}, u32[]{:S(2)}) copy-start(bf16[2048,2048]{1,0:T(8,128)(2,1)} %param.10) | copy-start | bytes 25165828
  62.5 10.1 %copy-start.4 = (bf16[1024,2048]{1,0:T(8,128)(2,1)S(1)}, bf16[1024,2048]{1,0:T(8,128)(2,1)}, u32[]{:S(2)}) copy-start(bf16[1024,2048]{1,0:T(8,128)(2,1)} %get-tuple-element.11) | copy-start | bytes 12582916
  83.6 89.8 %copy-start = (f32[256,512]{1,0:T(8,128)S(1)}, f32[256,512]{1,0:T(8,128)}, u32[]{:S(2)}) copy-start(f32[256,512]{1,0:T(8,128)} %param.13) | copy-start | bytes 1572868
  83.6 89.8 %copy-start.1 = (bf16[256,1024]{1,0:T(8,128)(2,1)S(1)}, bf16[256,1024]{1,0:T(8,128)(2,1)}, u32[]{:S(2)}) copy-start(bf16[256,1024]{1,0:T(8,128)(2,1)} %get-tuple-element.13) | copy-start | bytes 1572868
  175.8 8.2 %copy-start.2 = (f32[128,256]{1,0:T(8,128)S(1)}, f32[128,256]{1,0:T(8,128)}, u32[]{:S(2)}) copy-start(f32[128,256]{1,0:T(8,128)} %get-tuple-element.19) | copy-start | bytes 393220
Sparse Core Ops, SparseCore 0:
  62.6 24.4 all-gather.1
